TPU v7x, 32 devices: a whole 2x2x4 slice. The times are simulated.
32 devices in a mesh: pole: 4 (over x, core), row: 4 (over z), col: 2 (over y).
Axes of the slice: x: 2, y: 2, z: 4, core: 2. Of those that a mesh axis runs over, the one named last changes fastest.
Arguments:
- anc_inverse: bfloat16 [4, 2, 4, 192, 768], P('pole', None, None, 'col', 'row'), may hold values from -6 to 6
- panel: bfloat16 [4, 2, 768, 1024], P('pole', None, ('row', 'col')), may hold values from -0.21875 to 0.21875
- pattern: int32 [8, 2], replicated, may hold values 0 or 1
- diag_inverse: bfloat16 [4, 2, 1024, 512], P('pole', None, 'col', 'row'), may hold values from -6 to 6
- pole_weights: float32 [4, 2], P('pole'), may hold values from -4 to 4
Outputs:
- inv_panel: float32 [4, 2, 768, 1024], P('pole', None, 'row', 'col')
- inv_diag: bfloat16 [4, 2, 1024, 512], P('pole', None, 'col', 'row')
- density: float32 [1024, 512], P('col', 'row')
All inputs are finite; a program needn't handle non-finite values.
Results may differ from a plain program's by a relative error of at most 0.013.
Values may be sent and summed in bfloat16 or wider, within the bound.
A program may use at most 128 MiB of HBM per device.

v0:
```python
import jax
import jax.numpy as jnp
from jax import lax
from jax.sharding import PartitionSpec as P


def complex_left(left_re, left_im, right_re, right_im):
    upper = jnp.concatenate([left_re, left_im], axis=1)
    lower = jnp.concatenate([-left_im, left_re], axis=1)
    left_side = jnp.concatenate([upper, lower], axis=0)
    right_side = jnp.concatenate([right_re, right_im], axis=0)
    product = lax.dot_general(
        left_side, right_side, (((0,), (0,)), ((), ())), preferred_element_type=jnp.float32
    )
    return product.reshape(2, left_re.shape[1], right_re.shape[1])


def body(anc_inverse, panel, pattern, diag_inverse, pole_weights):
    n_row = lax.axis_size("row")
    n_col = lax.axis_size("col")
    fine_block = lax.axis_index("row") * n_col + lax.axis_index("col")
    pattern_row = lax.dynamic_slice_in_dim(pattern, fine_block, 1, 0)
    block_rows = panel.shape[2]
    width_all = panel.shape[3]
    groups = pattern.shape[1]
    keep_mask = pattern_row.astype(jnp.bfloat16).reshape(1, 1, 1, groups, 1)
    masked = (panel.reshape(1, 2, block_rows, groups, width_all // groups) * keep_mask).reshape(
        1, 2, block_rows, width_all
    )
    local_rows = lax.all_to_all(masked, "col", split_axis=3, concat_axis=2, tiled=True)
    row_count = anc_inverse.shape[4]
    col_count = local_rows.shape[3]
    full_cols = lax.all_gather(local_rows, "row", axis=2, tiled=True)
    stacked = full_cols[0].reshape(2, n_row, block_rows * n_col, col_count)
    segment = lax.all_gather(anc_inverse, "col", axis=3, tiled=True)
    length = segment.shape[3]
    left_side = segment[0].reshape(2, n_row * length, row_count)
    right_side = stacked.reshape(2, n_row * length, col_count)
    summed = complex_left(left_side[0], left_side[1], right_side[0], right_side[1])
    result_panel = -summed
    rounded = result_panel.astype(jnp.bfloat16)
    diag_terms = complex_left(local_rows[0, 0], local_rows[0, 1], rounded[0], rounded[1])
    row_share = lax.psum_scatter(diag_terms, "row", scatter_dimension=2, tiled=True)
    inverse_diag = diag_inverse[0].astype(jnp.float32) - row_share
    pole_weight = pole_weights[0]
    density_term = pole_weight[0] * inverse_diag[1] + pole_weight[1] * inverse_diag[0]
    density = lax.psum(density_term.astype(jnp.bfloat16), "pole").astype(jnp.float32)
    return (result_panel[None], inverse_diag.astype(jnp.bfloat16)[None], density)


def solution(mesh):
    placed = (
        P("pole", None, None, "col", "row"),
        P("pole", None, ("row", "col"), None),
        P(),
        P("pole", None, "col", "row"),
        P("pole", None),
    )
    return jax.shard_map(
        body,
        mesh=mesh,
        in_specs=placed,
        out_specs=(P("pole", None, "row", "col"), P("pole", None, "col", "row"), P("col", "row")),
        check_vma=False,
    )
```

profile of v0, /device:TPU:0, one launch (start us, length us, event | category | flops | bytes accessed | tf_op | source)
XLA Modules:
  0.0 151.4 jit_solution(4732061525736366362)
XLA Ops:
  7.2 0.0 all-gather.2.cloned.1.call-start
  7.2 0.9 fusion.26
  8.1 0.1 broadcast_bitcast_fusion
  8.2 1.0 broadcast_multiply_fusion
  9.2 0.4 copy.12
  9.6 12.2 %all_to_all.18 = bf16[1,2,96,1024]{2,1,0,3:T(2,128)(2,1)S(1)} all-to-all(bf16[1,2,96,1024]{2,1,0,3:T(2,128)(2,1)S(1)} %copy.12), channel_id=1, replica_groups=mesh['pole'=4,'row'=4,'col'=2] {'col'}, dimensions={3} | all-to-all | bytes 786432 | tf_op jit(solution)/shard_map/all_to_all | solution.py:30
  21.8 0.8 copy.15
  22.6 0.8 copy.14
  23.4 0.0 reduce-scatter.2.cloned.1.call-start
  23.5 10.5 %all_gather.6 = bf16[1,2,4,192,192]{4,3,2,1,0:T(8,128)(2,1)S(1)} all-gather(bf16[1,2,4,96,192]{4,3,2,1,0:T(8,128)(2,1)S(1)} %copy-done.1), channel_id=1, replica_groups=mesh['pole'=4,'row'=4,'col'=2] {'col'}, dimensions={3}, use_global_device_ids=true | all-gather | bytes 884736 | tf_op jit(solution)/shard_map/all_gather | solution.py:35
  34.0 0.1 fusion.30
  34.1 0.1 bitcast_negate_fusion
  34.2 26.8 %all-gather.2.cloned.1.call-done = bf16[1,2,768,512]{3,2,1,0:T(8,128)(2,1)} async-done(((bf16[1,2,192,512]{3,2,1,0:T(8,128)(2,1)}), bf16[1,2,768,512]{3,2,1,0:T(8,128)(2,1)}) %all-gather.2.cloned.1.call-update) | async-done | bytes 1572880 | tf_op jit(solution)/shard_map/all_gather | solution.py:33
  61.0 1.5 slice_bitcast_fusion.1
  62.5 1.1 fusion.4
  63.6 2.1 %fusion.14 = f32[1024,512]{1,0:T(8,128)} fusion(bf16[192,512]{1,0:T(8,128)(2,1)S(1)} %get-tuple-element.10, bf16[192,512]{1,0:T(8,128)(2,1)S(1)} %fusion.29, bf16[192,512]{1,0:T(8,128)(2,1)S(1)} %get-tuple-element.9, f32[384,512]{1,0:T(8,128)S(1)} %fusion.4), kind=kOutput, calls=%fused_computation.14 | convolution fusion | flops 405995520 | bytes 3473408 | tf_op jit(solution)/shard_map/dot_general | solution.py:12
  65.7 0.0 all-reduce.2.cloned.1.call-start
  65.8 0.6 copy-done.3
  66.3 0.6 fusion.31
  67.0 41.4 %reduce-scatter.2.cloned.1.call-done = f32[2,512,128]{2,1,0:T(8,128)} async-done(((f32[2,512,512]{2,1,0:T(8,128)}), f32[2,512,128]{2,1,0:T(8,128)}) %reduce-scatter.2.cloned.1.call-update) | async-done | bytes 524304 | tf_op jit(solution)/shard_map/reduce_scatter | solution.py:43
  108.4 1.8 %convert_bitcast_fusion = (bf16[1,2,512,128]{3,2,1,0:T(8,128)(2,1)}, f32[2,512,128]{2,1,0:T(8,128)S(1)}) fusion(f32[2,512,128]{2,1,0:T(8,128)} %reduce-scatter.2.cloned.1.call-done, bf16[1,2,512,128]{3,2,1,0:T(8,128)(2,1)S(1)} %copy-done.2), kind=kLoop, calls=%fused_computation.28 | loop fusion | flops 393216 | bytes 1572864 | tf_op jit(solution)/shard_map/broadcast_in_dim | solution.py:48
  110.2 1.9 %fusion.25 = bf16[512,128]{1,0:T(8,128)(2,1)} fusion(f32[2,512,128]{2,1,0:T(8,128)S(1)} %get-tuple-element.4, f32[]{:T(128)} %bitcast.14, f32[]{:T(128)} %bitcast.13), kind=kLoop, calls=%fused_computation.32 | loop fusion | flops 262144 | bytes 655368 | tf_op jit(solution)/shard_map/convert_element_type | solution.py:47
  112.1 31.1 %all-reduce.2.cloned.1.call-done = bf16[512,128]{1,0:T(8,128)(2,1)} async-done(((bf16[512,128]{1,0:T(8,128)(2,1)}), bf16[512,128]{1,0:T(8,128)(2,1)}) %all-reduce.2.cloned.1.call-update) | async-done | bytes 131088 | tf_op jit(solution)/shard_map/psum | solution.py:47
  143.2 1.6 %convert_element_type.32 = f32[512,128]{1,0:T(8,128)} convert(bf16[512,128]{1,0:T(8,128)(2,1)} %all-reduce.2.cloned.1.call-done) | non-fusion elementwise | flops 65536 | bytes 393216 | tf_op jit(solution)/shard_map/convert_element_type | solution.py:47
  (15 shorter events, 0.1 us)
Async XLA Ops:
  7.2 53.8 %all-gather.2.cloned.1.call-start = ((), (), s32[]{:S(2)}) async-start(), calls=%async_computation.2 | async-start | bytes 1966080 | tf_op jit(solution)/shard_map/all_gather | solution.py:33
  9.6 13.9 %copy-start.1 = (bf16[1,2,4,96,192]{4,3,2,1,0:T(8,128)(2,1)S(1)}, bf16[1,2,4,96,192]{4,3,2,1,0:T(8,128)(2,1)}, u32[]{:S(2)}) copy-start(bf16[1,2,4,96,192]{4,3,2,1,0:T(8,128)(2,1)} %param.5) | copy-start | bytes 884740
  23.4 10.7 %copy-start = (bf16[1,2,2,96,512]{4,3,2,1,0:T(8,128)(2,1)S(1)}, bf16[1,2,2,96,512]{4,3,2,1,0:T(8,128)(2,1)}, u32[]{:S(2)}) copy-start(bf16[1,2,2,96,512]{4,3,2,1,0:T(8,128)(2,1)} %copy.14) | copy-start | bytes 1179652
  23.4 84.9 %reduce-scatter.2.cloned.1.call-start = ((), (), s32[]{:S(2)}) async-start(), calls=%async_computation.3 | async-start | bytes 2621440 | tf_op jit(solution)/shard_map/reduce_scatter | solution.py:43
  63.6 2.1 %copy-start.4 = (f32[384,512]{1,0:T(8,128)}, f32[384,512]{1,0:T(8,128)S(1)}, u32[]{:S(2)}) copy-start(f32[384,512]{1,0:T(8,128)S(1)} %fusion.4) | copy-start | bytes 2359300
  65.7 0.7 copy-start.3
  65.7 42.7 %copy-start.2 = (bf16[1,2,512,128]{3,2,1,0:T(8,128)(2,1)S(1)}, bf16[1,2,512,128]{3,2,1,0:T(8,128)(2,1)}, u32[]{:S(2)}) copy-start(bf16[1,2,512,128]{3,2,1,0:T(8,128)(2,1)} %param.8) | copy-start | bytes 786436
  65.7 77.5 %all-reduce.2.cloned.1.call-start = ((), (), s32[]{:S(2)}) async-start(), calls=%async_computation.4 | async-start | bytes 262144 | tf_op jit(solution)/shard_map/psum | solution.py:47
Sparse Core Ops, SparseCore 0:
  23.5 37.4 all-gather.1
  65.8 42.5 reduce-scatter.1
  112.2 30.9 all-reduce.1
where the time goes:
time: 152 us; the launch traced here: 151 us
  waiting for transfers between devices  99.4 us (65%)
  blocking collectives  22.7 us (15%)
  between operations  13.8 us (9%)
  other arithmetic  7.29 us (5%)
  local copies, waits for them, and re-layouts  4.86 us (3%)
  matrix products  3.19 us (2%)
    reduce_scatter x1, waiting for transfers between devices, body(): lax.psum_scatter(diag_terms, 'row', scatter_dimension=2, tiled=True)  41.4 us
    psum x1, waiting for transfers between devices, body(): lax.psum(density_term.astype(jnp.bfloat16), 'pole').astype(jnp.float32)  31.1 us
    all_gather x1, waiting for transfers between devices, body(): full_cols = lax.all_gather(local_rows, 'row', axis=2, tiled=True)  26.8 us
    all_to_all x1, blocking collectives, body(): lax.all_to_all(masked, 'col', split_axis=3, concat_axis=2, tiled=True)  12.2 us
    all_gather x1, blocking collectives, body(): segment = lax.all_gather(anc_inverse, 'col', axis=3, tiled=True)  10.5 us
    dot_general x2, matrix products, complex_left(): lax.dot_general(left_side, right_side, (((0,), (0,)), ((), ())), preferre...  3.19 us
  transfers between devices with their start and end apart: 3, of which 3 were waited for; matrix products, arithmetic and copies ran while one was open for 1% of the time, Pallas kernels for 0%

commit v1 on v0

--- a/solution.py
+++ b/solution.py
@@ -2,6 +2,12 @@
 import jax.numpy as jnp
 from jax import lax
 from jax.sharding import PartitionSpec as P
+
+
+def gather_and_add(shard, axis):
+    terms = lax.all_gather(shard, axis, axis=0, tiled=False)
+    total = terms.sum(axis=0)
+    return total
 
 
 def complex_left(left_re, left_im, right_re, right_im):
@@ -44,7 +50,7 @@
     inverse_diag = diag_inverse[0].astype(jnp.float32) - row_share
     pole_weight = pole_weights[0]
     density_term = pole_weight[0] * inverse_diag[1] + pole_weight[1] * inverse_diag[0]
-    density = lax.psum(density_term.astype(jnp.bfloat16), "pole").astype(jnp.float32)
+    density = gather_and_add(density_term.astype(jnp.bfloat16), "pole").astype(jnp.float32)
     return (result_panel[None], inverse_diag.astype(jnp.bfloat16)[None], density)
 
 

time: 152 us -> 127 us (0.84)
  waiting for transfers between devices: 99.4 us -> 68.2 us
  blocking collectives: 22.7 us -> 29.8 us
    psum x1 -> x0, waiting for transfers between devices: 31.1 us -> none  [body(): lax.psum(density_term.astype(jnp.bfloat16), 'pole').astype(jnp.float32)]
    all_gather x0 -> x1, blocking collectives: none -> 7.13 us  [gather_and_add(): terms = lax.all_gather(shard, axis, axis=0, tiled=False)]
  transfers between devices with their start and end apart: 3 -> 2, of which waited for: 3 -> 2; matrix products, arithmetic and copies ran while one was open for 1% -> 1% of each run, Pallas kernels for 0% -> 0%
where the time goes in v1:
time: 127 us; the launch traced here: 126 us
  waiting for transfers between devices  68.2 us (54%)
  blocking collectives  29.8 us (23%)
  between operations  14.2 us (11%)
  other arithmetic  5.94 us (5%)
  local copies, waits for them, and re-layouts  4.94 us (4%)
  matrix products  3.2 us (3%)
    reduce_scatter x1, waiting for transfers between devices, body(): lax.psum_scatter(diag_terms, 'row', scatter_dimension=2, tiled=True)  41.4 us
    all_gather x1, waiting for transfers between devices, body(): full_cols = lax.all_gather(local_rows, 'row', axis=2, tiled=True)  26.8 us
    all_to_all x1, blocking collectives, body(): lax.all_to_all(masked, 'col', split_axis=3, concat_axis=2, tiled=True)  12.2 us
    all_gather x1, blocking collectives, body(): segment = lax.all_gather(anc_inverse, 'col', axis=3, tiled=True)  10.5 us
    all_gather x1, blocking collectives, gather_and_add(): terms = lax.all_gather(shard, axis, axis=0, tiled=False)  7.13 us
    dot_general x2, matrix products, complex_left(): lax.dot_general(left_side, right_side, (((0,), (0,)), ((), ())), preferre...  3.2 us
  transfers between devices with their start and end apart: 2, of which 2 were waited for; matrix products, arithmetic and copies ran while one was open for 1% of the time, Pallas kernels for 0%

profile of v1, /device:TPU:0, one launch (start us, length us, event | category | flops | bytes accessed | tf_op | source)
XLA Modules:
  0.0 126.3 jit_solution(17357969155942034795)
XLA Ops:
  7.2 0.0 all-gather.2.cloned.1.call-start
  7.2 0.9 fusion.25
  8.1 0.1 broadcast_bitcast_fusion
  8.2 1.0 broadcast_multiply_fusion
  9.2 0.4 copy.12
  9.6 12.2 %all_to_all.18 = bf16[1,2,96,1024]{2,1,0,3:T(2,128)(2,1)S(1)} all-to-all(bf16[1,2,96,1024]{2,1,0,3:T(2,128)(2,1)S(1)} %copy.12), channel_id=1, replica_groups=mesh['pole'=4,'row'=4,'col'=2] {'col'}, dimensions={3} | all-to-all | bytes 786432 | tf_op jit(solution)/shard_map/all_to_all | solution.py:36
  21.8 0.8 copy.15
  22.6 0.8 copy.14
  23.4 0.0 reduce-scatter.2.cloned.1.call-start
  23.5 10.5 %all_gather.10 = bf16[1,2,4,192,192]{4,3,2,1,0:T(8,128)(2,1)S(1)} all-gather(bf16[1,2,4,96,192]{4,3,2,1,0:T(8,128)(2,1)S(1)} %copy-done.1), channel_id=1, replica_groups=mesh['pole'=4,'row'=4,'col'=2] {'col'}, dimensions={3}, use_global_device_ids=true | all-gather | bytes 884736 | tf_op jit(solution)/shard_map/all_gather | solution.py:41
  34.0 0.1 fusion.29
  34.1 0.1 bitcast_negate_fusion
  34.2 26.8 %all-gather.2.cloned.1.call-done = bf16[1,2,768,512]{3,2,1,0:T(8,128)(2,1)} async-done(((bf16[1,2,192,512]{3,2,1,0:T(8,128)(2,1)}), bf16[1,2,768,512]{3,2,1,0:T(8,128)(2,1)}) %all-gather.2.cloned.1.call-update) | async-done | bytes 1572880 | tf_op jit(solution)/shard_map/all_gather | solution.py:39
  61.0 1.5 %slice_bitcast_fusion.1 = (bf16[768,512]{1,0:T(8,128)(2,1)S(1)}, bf16[768,512]{1,0:T(8,128)(2,1)S(1)}) fusion(bf16[1,2,768,512]{3,2,1,0:T(8,128)(2,1)} %all-gather.2.cloned.1.call-done), kind=kLoop, calls=%fused_computation.13 | loop fusion | bytes 3145728 | tf_op jit(solution)/shard_map/squeeze | solution.py:45
  62.5 1.1 fusion.4
  63.6 2.1 %fusion.14 = f32[1024,512]{1,0:T(8,128)} fusion(bf16[192,512]{1,0:T(8,128)(2,1)S(1)} %get-tuple-element.10, bf16[192,512]{1,0:T(8,128)(2,1)S(1)} %fusion.28, bf16[192,512]{1,0:T(8,128)(2,1)S(1)} %get-tuple-element.9, f32[384,512]{1,0:T(8,128)S(1)} %fusion.4), kind=kOutput, calls=%fused_computation.14 | convolution fusion | flops 405995520 | bytes 3473408 | tf_op jit(solution)/shard_map/dot_general | solution.py:18
  65.7 0.6 copy-done.3
  66.4 0.6 fusion.30
  67.0 41.4 %reduce-scatter.2.cloned.1.call-done = f32[2,512,128]{2,1,0:T(8,128)} async-done(((f32[2,512,512]{2,1,0:T(8,128)}), f32[2,512,128]{2,1,0:T(8,128)}) %reduce-scatter.2.cloned.1.call-update) | async-done | bytes 524304 | tf_op jit(solution)/shard_map/reduce_scatter | solution.py:49
  108.4 1.8 %convert_bitcast_fusion = (bf16[1,2,512,128]{3,2,1,0:T(8,128)(2,1)}, f32[2,512,128]{2,1,0:T(8,128)S(1)}) fusion(f32[2,512,128]{2,1,0:T(8,128)} %reduce-scatter.2.cloned.1.call-done, bf16[1,2,512,128]{3,2,1,0:T(8,128)(2,1)S(1)} %copy-done.2), kind=kLoop, calls=%fused_computation.28 | loop fusion | flops 393216 | bytes 1572864 | tf_op jit(solution)/shard_map/broadcast_in_dim | solution.py:54
  110.2 1.4 %fusion.24 = bf16[1,512,128]{2,1,0:T(8,128)(2,1)S(1)} fusion(f32[2,512,128]{2,1,0:T(8,128)S(1)} %get-tuple-element.4, f32[]{:T(128)} %bitcast.14, f32[]{:T(128)} %bitcast.13), kind=kLoop, calls=%fused_computation.26 | loop fusion | flops 262144 | bytes 655368 | tf_op jit(solution)/shard_map/convert_element_type | solution.py:53
  111.6 7.1 %all_gather.12 = bf16[4,512,128]{2,1,0:T(8,128)(2,1)S(1)} all-gather(bf16[1,512,128]{2,1,0:T(8,128)(2,1)S(1)} %fusion.24), channel_id=1, replica_groups=mesh['pole'=4,'row'=4,'col'=2] {'pole'}, dimensions={0}, use_global_device_ids=true | all-gather | bytes 655360 | tf_op jit(solution)/shard_map/all_gather | solution.py:8
  118.7 0.1 reduce_sum.12
  118.8 0.7 convert_element_type.31
  (14 shorter events, 0.1 us)
Async XLA Ops:
  7.2 53.8 %all-gather.2.cloned.1.call-start = ((), (), s32[]{:S(2)}) async-start(), calls=%async_computation.2 | async-start | bytes 1966080 | tf_op jit(solution)/shard_map/all_gather | solution.py:39
  9.6 13.9 %copy-start.1 = (bf16[1,2,4,96,192]{4,3,2,1,0:T(8,128)(2,1)S(1)}, bf16[1,2,4,96,192]{4,3,2,1,0:T(8,128)(2,1)}, u32[]{:S(2)}) copy-start(bf16[1,2,4,96,192]{4,3,2,1,0:T(8,128)(2,1)} %param.5) | copy-start | bytes 884740
  23.4 10.7 %copy-start = (bf16[1,2,2,96,512]{4,3,2,1,0:T(8,128)(2,1)S(1)}, bf16[1,2,2,96,512]{4,3,2,1,0:T(8,128)(2,1)}, u32[]{:S(2)}) copy-start(bf16[1,2,2,96,512]{4,3,2,1,0:T(8,128)(2,1)} %copy.14) | copy-start | bytes 1179652
  23.4 85.0 %reduce-scatter.2.cloned.1.call-start = ((), (), s32[]{:S(2)}) async-start(), calls=%async_computation.3 | async-start | bytes 2621440 | tf_op jit(solution)/shard_map/reduce_scatter | solution.py:49
  63.6 2.1 %copy-start.4 = (f32[384,512]{1,0:T(8,128)}, f32[384,512]{1,0:T(8,128)S(1)}, u32[]{:S(2)}) copy-start(f32[384,512]{1,0:T(8,128)S(1)} %fusion.4) | copy-start | bytes 2359300
  65.7 0.7 copy-start.3
  65.7 42.7 %copy-start.2 = (bf16[1,2,512,128]{3,2,1,0:T(8,128)(2,1)S(1)}, bf16[1,2,512,128]{3,2,1,0:T(8,128)(2,1)}, u32[]{:S(2)}) copy-start(bf16[1,2,512,128]{3,2,1,0:T(8,128)(2,1)} %param.8) | copy-start | bytes 786436
Sparse Core Ops, SparseCore 0:
  23.5 37.4 all-gather.1
  65.9 42.5 reduce-scatter.1
